TPU v7x, 128 devices: a whole 4x4x4 slice. The times are simulated.
128 devices in a mesh: dom: 128 (over y, z, x, core).
Axes of the slice: x: 4, y: 4, z: 4, core: 2. Of those that a mesh axis runs over, the one named last changes fastest.
Arguments:
- right_side: float32 [131072, 3], P('dom'), may hold values from -10 to 10
- fine_diagonal: float32 [131072, 3], P('dom'), may hold values from 2 to 4
- fine_columns: int32 [131072, 27], P('dom'), may hold values from 0 to 131071, as said below
- fine_blocks: float32 [131072, 27, 3, 3], P('dom'), may hold values from -0.625 to 0.625
- aggregate_of_node: int32 [131072], P('dom'), may hold values from 0 to 31, as said below
- coarse_row_of_aggregate: int32 [4096], P('dom'), may hold values from 0 to 4095, as said below
- coarse_diagonal: float32 [4096, 3], P('dom'), may hold values from 2 to 4
- coarse_columns: int32 [4096, 27], P('dom'), may hold values from 0 to 4095
- coarse_blocks: float32 [4096, 27, 3, 3], P('dom'), may hold values from -0.625 to 0.625
Outputs:
- solution: float32 [131072, 3], P('dom')
- correction: float32 [4096, 3], P('dom')
Inputs may be any that keep to these rules, and one draw needn't show every extreme that they name: Every entry of fine_columns differs from its row number by at most 256, and some entry by exactly 256. `aggregate_of_node`: on each device every aggregate number 0 to 31 is used by at least one of its nodes. coarse_row_of_aggregate is a permutation of 0 to 4095; among the 32 aggregates of one device (an aligned block of entries) at most 8 get rows of any one owner, and exactly 8 for some owner.
All inputs are finite; a program needn't handle non-finite values.
Results may differ from a plain program's by a relative error of at most 0.0003.
Values sent between devices are 32-bit elements.
A program may use at most 64 MiB of HBM per device.

v0:
```python
import jax
import jax.numpy as jnp
from jax import lax
from jax.sharding import Mesh
from jax.sharding import PartitionSpec as P

CAP = 8
WIN = 256
SWEEPS = 2
CSWEEPS = 6
DOM = ("dom_0", "dom_1", "dom_2", "dom_3")
damping = 0.7
highest = lax.Precision.HIGHEST


def padded_2(value, sides, width, wrap):
    for axis, dim in sides:
        peers, length = (lax.axis_size(axis), value.shape[dim])
        up = [(i, (i + 1) % peers) for i in range(peers if wrap else peers - 1)]
        down = [(j, i) for i, j in up]
        last = lax.slice_in_dim(value, length - width, length, axis=dim)
        initial = lax.slice_in_dim(value, 0, width, axis=dim)
        before = lax.ppermute(last, axis, up)
        after = lax.ppermute(initial, axis, down)
        value = jnp.concatenate([before, value, after], axis=dim)
    return value


def split_up(value, dim, peers):
    return jnp.stack(jnp.split(value, peers, axis=dim))


def joined_along(tiles, dim):
    tiles = jnp.moveaxis(tiles, 0, dim)
    shape = tiles.shape
    return tiles.reshape(*shape[:dim], shape[dim] * shape[dim + 1], *shape[dim + 2 :])


def turned_blocks(tiles, axes, sequence):
    inside = tiles.shape[1:]
    whole = tiles.reshape(*(lax.axis_size(a) for a in axes), *inside)
    for k in sequence:
        whole = lax.all_to_all(whole, axes[k], k, k, tiled=True)
    return whole.reshape(-1, *inside)


def exchange_by_chip(value, groups, sequence, split_dim, concat_dim):
    peers = lax.axis_size(groups[0]) * lax.axis_size(groups[1])
    tiles = split_up(value, split_dim, peers)
    return joined_along(turned_blocks(tiles, groups, sequence), concat_dim)


def couple(blocks, nearby):
    return jnp.sum(blocks * nearby[:, :, None, :], axis=(1, 3))


def apply_fine(field, fine_diagonal, fine_columns, fine_blocks):
    row_count = fine_columns.shape[0]
    padded = padded_2(field, ((DOM, 0),), WIN, False)
    first_row = lax.axis_index(DOM) * row_count - WIN
    local_columns = (fine_columns - first_row).astype(jnp.int32)
    nearby = padded[local_columns]
    return fine_diagonal * field - couple(fine_blocks, nearby)


def apply_coarse(field, coarse_diagonal, coarse_columns, coarse_blocks):
    gathered = lax.all_gather(field, DOM, axis=0, tiled=True)
    nearby = gathered[coarse_columns]
    return coarse_diagonal * field - couple(coarse_blocks, nearby)


def body(
    right_side,
    fine_diagonal,
    fine_columns,
    fine_blocks,
    aggregate_of_node,
    coarse_row_of_aggregate,
    coarse_diagonal,
    coarse_columns,
    coarse_blocks,
):
    solution = damping * right_side / fine_diagonal
    for sweep in range(SWEEPS - 1):
        solution = (
            solution
            + damping
            * (right_side - apply_fine(solution, fine_diagonal, fine_columns, fine_blocks))
            / fine_diagonal
        )
    residual = right_side - apply_fine(solution, fine_diagonal, fine_columns, fine_blocks)
    aggregate_count = coarse_diagonal.shape[0]
    devices = lax.axis_size(DOM)
    aggregate_ids = jnp.arange(aggregate_count, dtype=jnp.int32)
    sums_here = jax.ops.segment_sum(residual, aggregate_of_node, num_segments=aggregate_count)
    owners = coarse_row_of_aggregate // aggregate_count
    member = (owners[:, None] == jnp.arange(devices, dtype=jnp.int32)[None, :]).astype(jnp.float32)
    earlier = (aggregate_ids[None, :] < aggregate_ids[:, None]).astype(jnp.float32)
    before = jnp.dot(earlier, member, precision=highest)
    position = jnp.sum(before * member, axis=1).astype(jnp.int32)
    bucket = (owners * CAP + position).astype(jnp.int32)
    local_rows = (coarse_row_of_aggregate - owners * aggregate_count).astype(jnp.int32)
    slot_out = jnp.full((devices * CAP,), aggregate_count, jnp.int32).at[bucket].set(local_rows)
    slot_in = exchange_by_chip(slot_out, (("dom_0", "dom_1", "dom_2"), "dom_3"), (0, 1), 0, 0)
    outgoing = jnp.zeros((devices * CAP, 3), jnp.float32).at[bucket].set(sums_here)
    arrived = exchange_by_chip(outgoing, (("dom_0", "dom_1", "dom_2"), "dom_3"), (0, 1), 0, 0)
    coarse_rhs = jnp.zeros((aggregate_count, 3), jnp.float32).at[slot_in].add(arrived, mode="drop")
    correction = damping * coarse_rhs / coarse_diagonal
    for sweep in range(CSWEEPS - 1):
        correction = (
            correction
            + damping
            * (
                coarse_rhs
                - apply_coarse(correction, coarse_diagonal, coarse_columns, coarse_blocks)
            )
            / coarse_diagonal
        )
    sending = jnp.take(correction, slot_in, axis=0, mode="fill", fill_value=0.0)
    returned = exchange_by_chip(sending, (("dom_0", "dom_1", "dom_2"), "dom_3"), (0, 1), 0, 0)
    label_values = returned[bucket]
    solution = solution + label_values[aggregate_of_node]
    for sweep in range(SWEEPS):
        solution = (
            solution
            + damping
            * (right_side - apply_fine(solution, fine_diagonal, fine_columns, fine_blocks))
            / fine_diagonal
        )
    return (solution, correction)


def solution(mesh):
    torus = Mesh(mesh.devices.reshape(4, 4, 4, 2), ("dom_0", "dom_1", "dom_2", "dom_3"))
    return jax.shard_map(
        body,
        mesh=torus,
        in_specs=(
            P(DOM, None),
            P(DOM, None),
            P(DOM, None),
            P(DOM, None, None, None),
            P(DOM),
            P(DOM),
            P(DOM, None),
            P(DOM, None),
            P(DOM, None, None, None),
        ),
        out_specs=(P(DOM, None), P(DOM, None)),
        check_vma=False,
    )
```

profile of v0, /device:TPU:103, one launch (start us, length us, event | category | flops | bytes accessed | tf_op | source)
XLA Modules:
  0.0 762.8 jit_solution(1142505852747501974)
XLA Ops:
  8.2 9.7 %stack.1289 = s32[128,8]{1,0:T(8,128)} concatenate(s32[1,8]{1,0:T(1,128)S(1)} %get-tuple-element.405, s32[1,8]{1,0:T(1,128)S(1)} %get-tuple-element.404, s32[1,8]{1,0:T(1,128)S(1)} %get-tuple-element.403, s32[1,8]{1,0:T(1,128)S(1)} %get-tuple-element.402, s32[1,8]{1,0:T(1,128)S(1)} %get-tuple-element.401, s32[1,8]{1,0:T(1,128)S(1)} %get-tuple-element.400, ...), dimensions={0} | concatenate | bytes 8192 | tf_op jit(solution)/shard_map/stack | solution.py:30
  17.9 10.3 %all-to-all-start = ((s32[64,2,8]{2,1,0:T(2,128)}), s32[64,2,8]{2,1,0:T(2,128)S(1)}, u32[]{:S(2)}, u32[]{:S(2)}) async-start(s32[64,2,8]{2,1,0:T(2,128)} %bitcast.128), calls=%async_computation | async-start | bytes 131072 | tf_op jit(solution)/shard_map/all_to_all | solution.py:43
  30.3 91.5 %gather_fusion = f32[27648,3]{1,0:T(8,128)} fusion(f32[1536,3]{1,0:T(8,128)S(1)} %copy.2716, s32[27648]{0:T(1024)S(1)} %broadcast_clamp_fusion), kind=kCustom, calls=%fused_computation | custom fusion | bytes 774144 | tf_op jit(solution)/shard_map/gather | solution.py:62
  121.8 8.3 %copy.2717 = f32[27648,3]{0,1:T(4,128)S(1)} copy(f32[27648,3]{1,0:T(8,128)} %gather_fusion) | data formatting | bytes 663552 | tf_op jit(solution)/shard_map/gather | solution.py:62
  149.1 91.5 %gather_fusion.1 = f32[27648,3]{1,0:T(8,128)} fusion(f32[1536,3]{1,0:T(8,128)S(1)} %copy.2722, s32[27648]{0:T(1024)S(1)} %broadcast_clamp_fusion), kind=kCustom, calls=%fused_computation.1 | custom fusion | bytes 774144 | tf_op jit(solution)/shard_map/gather | solution.py:62
  240.7 8.3 %copy.2723 = f32[27648,3]{0,1:T(4,128)S(1)} copy(f32[27648,3]{1,0:T(8,128)} %gather_fusion.1) | data formatting | bytes 663552 | tf_op jit(solution)/shard_map/gather | solution.py:62
  254.3 6.0 scatter_custom_fusion.1
  274.1 8.9 %all-to-all-start.2 = ((f32[64,2,8,3]{2,1,3,0:T(2,128)}), f32[64,2,8,3]{2,1,3,0:T(2,128)S(1)}, u32[]{:S(2)}, u32[]{:S(2)}) async-start(f32[64,2,8,3]{2,1,3,0:T(2,128)} %copy.2855), calls=%async_computation.2 | async-start | bytes 393216 | tf_op jit(solution)/shard_map/all_to_all | solution.py:43
  283.1 6.5 all-to-all-done.2
  296.2 6.0 scatter_custom_fusion.3
  302.3 34.5 %all-gather = f32[128,32,3]{1,2,0:T(4,128)S(1)} all-gather(f32[1,32,3]{1,2,0:T(4,128)S(1)} %fusion.11), channel_id=1, replica_groups=mesh['dom_0'=4,'dom_1'=4,'dom_2'=4,'dom_3'=2] {'dom_0','dom_1','dom_2','..., dimensions={0}, use_global_device_ids=true | all-gather | bytes 49536 | tf_op jit(solution)/shard_map/all_gather | solution.py:67
  340.0 33.4 %all-gather.1 = f32[128,32,3]{1,2,0:T(4,128)S(1)} all-gather(f32[1,32,3]{1,2,0:T(4,128)S(1)} %bitcast.827), channel_id=1, replica_groups=mesh['dom_0'=4,'dom_1'=4,'dom_2'=4,'dom_3'=2] {'dom_0','dom_1','dom_2','..., dimensions={0}, use_global_device_ids=true | all-gather | bytes 49536 | tf_op jit(solution)/shard_map/all_gather | solution.py:67
  376.5 33.4 %all-gather.2 = f32[128,32,3]{1,2,0:T(4,128)S(1)} all-gather(f32[1,32,3]{1,2,0:T(4,128)S(1)} %bitcast.825), channel_id=1, replica_groups=mesh['dom_0'=4,'dom_1'=4,'dom_2'=4,'dom_3'=2] {'dom_0','dom_1','dom_2','..., dimensions={0}, use_global_device_ids=true | all-gather | bytes 49536 | tf_op jit(solution)/shard_map/all_gather | solution.py:67
  413.0 33.6 %all-gather.3 = f32[128,32,3]{1,2,0:T(4,128)S(1)} all-gather(f32[1,32,3]{1,2,0:T(4,128)S(1)} %bitcast.826), channel_id=1, replica_groups=mesh['dom_0'=4,'dom_1'=4,'dom_2'=4,'dom_3'=2] {'dom_0','dom_1','dom_2','..., dimensions={0}, use_global_device_ids=true | all-gather | bytes 49536 | tf_op jit(solution)/shard_map/all_gather | solution.py:67
  449.8 33.4 %all-gather.4 = f32[128,32,3]{1,2,0:T(4,128)S(1)} all-gather(f32[1,32,3]{1,2,0:T(4,128)S(1)} %bitcast.824), channel_id=1, replica_groups=mesh['dom_0'=4,'dom_1'=4,'dom_2'=4,'dom_3'=2] {'dom_0','dom_1','dom_2','..., dimensions={0}, use_global_device_ids=true | all-gather | bytes 49536 | tf_op jit(solution)/shard_map/all_gather | solution.py:67
  502.2 7.5 all-to-all-start.4
  509.8 6.3 all-to-all-done.4
  526.0 5.5 collective-permute-start.4
  533.5 7.2 collective-permute-done.5
  541.0 91.5 %gather_fusion.10 = f32[27648,3]{1,0:T(8,128)} fusion(f32[1536,3]{1,0:T(8,128)S(1)} %copy.3009, s32[27648]{0:T(1024)S(1)} %broadcast_clamp_fusion), kind=kCustom, calls=%fused_computation.10 | custom fusion | bytes 774144 | tf_op jit(solution)/shard_map/gather | solution.py:62
  632.5 8.3 %copy.3010 = f32[27648,3]{0,1:T(4,128)S(1)} copy(f32[27648,3]{1,0:T(8,128)} %gather_fusion.10) | data formatting | bytes 663552 | tf_op jit(solution)/shard_map/gather | solution.py:62
  650.5 6.5 collective-permute-done.7
  657.3 91.5 %gather_fusion.11 = f32[27648,3]{1,0:T(8,128)} fusion(f32[1536,3]{1,0:T(8,128)S(1)} %copy.3012, s32[27648]{0:T(1024)S(1)} %broadcast_clamp_fusion), kind=kCustom, calls=%fused_computation.11 | custom fusion | bytes 774144 | tf_op jit(solution)/shard_map/gather | solution.py:62
  748.8 8.3 %copy.3013 = f32[27648,3]{0,1:T(4,128)S(1)} copy(f32[27648,3]{1,0:T(8,128)} %gather_fusion.11) | data formatting | bytes 663552 | tf_op jit(solution)/shard_map/gather | solution.py:62
  (674 shorter events, 112.6 us)
Async XLA Ops:
  0.6 29.2 %copy-start.6 = (s32[32,27]{1,0:T(8,128)S(1)}, s32[32,27]{1,0:T(8,128)}, u32[]{:S(2)}) copy-start(s32[32,27]{1,0:T(8,128)} %param.16) | copy-start | bytes 10372
  1.4 28.5 %collective-permute-start = (f32[256,3]{0,1:T(4,128)S(1)}, f32[256,3]{0,1:T(4,128)S(1)}, u32[]{:S(2)}, u32[]{:S(2)}) collective-permute-start(f32[256,3]{0,1:T(4,128)S(1)} %get-tuple-element.276), channel_id=1, source_target_pairs={{0,1},{1,2},{2,3},{3,4},{4,5},{5,6},{6,7},{7,8},{8,9},{9,10},{10,1... | collective-permute-start | bytes 9224 | tf_op jit(solution)/shard_map/ppermute | solution.py:23
  3.7 26.2 %collective-permute-start.1 = (f32[256,3]{0,1:T(4,128)S(1)}, f32[256,3]{0,1:T(4,128)S(1)}, u32[]{:S(2)}, u32[]{:S(2)}) collective-permute-start(f32[256,3]{0,1:T(4,128)S(1)} %get-tuple-element.277), channel_id=1, source_target_pairs={{1,0},{2,1},{3,2},{4,3},{5,4},{6,5},{7,6},{8,7},{9,8},{10,9},{11,1... | collective-permute-start | bytes 9224 | tf_op jit(solution)/shard_map/ppermute | solution.py:24
  17.9 123.7 %all-to-all-start = ((s32[64,2,8]{2,1,0:T(2,128)}), s32[64,2,8]{2,1,0:T(2,128)S(1)}, u32[]{:S(2)}, u32[]{:S(2)}) async-start(s32[64,2,8]{2,1,0:T(2,128)} %bitcast.128), calls=%async_computation | async-start | bytes 131072 | tf_op jit(solution)/shard_map/all_to_all | solution.py:43
  130.1 4.9 copy-start
  133.1 2.1 copy-start.3
  133.1 2.1 copy-start.4
  135.2 12.3 %collective-permute-start.2 = (f32[256,3]{0,1:T(4,128)S(1)}, f32[256,3]{0,1:T(4,128)S(1)}, u32[]{:S(2)}, u32[]{:S(2)}) collective-permute-start(f32[256,3]{0,1:T(4,128)S(1)} %get-tuple-element.274), channel_id=1, source_target_pairs={{0,1},{1,2},{2,3},{3,4},{4,5},{5,6},{6,7},{7,8},{8,9},{9,10},{10,1... | collective-permute-start | bytes 9224 | tf_op jit(solution)/shard_map/ppermute | solution.py:23
  139.7 9.1 %collective-permute-start.3 = (f32[256,3]{0,1:T(4,128)S(1)}, f32[256,3]{0,1:T(4,128)S(1)}, u32[]{:S(2)}, u32[]{:S(2)}) collective-permute-start(f32[256,3]{0,1:T(4,128)S(1)} %get-tuple-element.275), channel_id=1, source_target_pairs={{1,0},{2,1},{3,2},{4,3},{5,4},{6,5},{7,6},{8,7},{9,8},{10,9},{11,1... | collective-permute-start | bytes 9224 | tf_op jit(solution)/shard_map/ppermute | solution.py:24
  251.9 2.3 copy-start.8
  261.3 41.0 %copy-start.5 = (f32[32,3]{0,1:T(4,128)S(1)}, f32[32,3]{0,1:T(4,128)}, u32[]{:S(2)}) copy-start(f32[32,3]{0,1:T(4,128)} %param.15) | copy-start | bytes 1156
  274.1 15.4 %all-to-all-start.2 = ((f32[64,2,8,3]{2,1,3,0:T(2,128)}), f32[64,2,8,3]{2,1,3,0:T(2,128)S(1)}, u32[]{:S(2)}, u32[]{:S(2)}) async-start(f32[64,2,8,3]{2,1,3,0:T(2,128)} %copy.2855), calls=%async_computation.2 | async-start | bytes 393216 | tf_op jit(solution)/shard_map/all_to_all | solution.py:43
  337.7 2.2 copy-start.2
  486.3 2.9 copy-start.7
  502.2 13.8 %all-to-all-start.4 = ((f32[64,2,8,3]{2,1,3,0:T(2,128)}), f32[64,2,8,3]{2,1,3,0:T(2,128)S(1)}, u32[]{:S(2)}, u32[]{:S(2)}) async-start(f32[64,2,8,3]{2,1,3,0:T(2,128)} %copy.3005), calls=%async_computation.4 | async-start | bytes 393216 | tf_op jit(solution)/shard_map/all_to_all | solution.py:43
  526.0 7.4 collective-permute-start.4
  531.5 9.1 %collective-permute-start.5 = (f32[256,3]{0,1:T(4,128)S(1)}, f32[256,3]{0,1:T(4,128)S(1)}, u32[]{:S(2)}, u32[]{:S(2)}) collective-permute-start(f32[256,3]{0,1:T(4,128)S(1)} %get-tuple-element.273), channel_id=1, source_target_pairs={{1,0},{2,1},{3,2},{4,3},{5,4},{6,5},{7,6},{8,7},{9,8},{10,9},{11,1... | collective-permute-start | bytes 9224 | tf_op jit(solution)/shard_map/ppermute | solution.py:24
  640.8 4.9 copy-start.1
  645.9 4.6 collective-permute-start.6
  647.8 9.1 %collective-permute-start.7 = (f32[256,3]{0,1:T(4,128)S(1)}, f32[256,3]{0,1:T(4,128)S(1)}, u32[]{:S(2)}, u32[]{:S(2)}) collective-permute-start(f32[256,3]{0,1:T(4,128)S(1)} %get-tuple-element.271), channel_id=1, source_target_pairs={{1,0},{2,1},{3,2},{4,3},{5,4},{6,5},{7,6},{8,7},{9,8},{10,9},{11,1... | collective-permute-start | bytes 9224 | tf_op jit(solution)/shard_map/ppermute | solution.py:24
where the time goes:
time: 764 us; the launch traced here: 763 us
  local copies, waits for them, and re-layouts  482 us (63%)
  blocking collectives  182 us (24%)
  starting transfers between devices  49.7 us (7%)
  waiting for transfers between devices  27.8 us (4%)
  other arithmetic  18.7 us (2%)
    gather x16, local copies, waits for them, and re-layouts, apply_fine(): nearby = padded[local_columns]  419 us
    all_gather x5, blocking collectives, apply_coarse(): gathered = lax.all_gather(field, DOM, axis=0, tiled=True)  168 us
    all_to_all x3, starting transfers between devices, turned_blocks(): whole = lax.all_to_all(whole, axes[k], k, k, tiled=True)  26.8 us
    split x270, local copies, waits for them, and re-layouts, split_up(): return jnp.stack(jnp.split(value, peers, axis=dim))  20.8 us
  transfers between devices with their start and end apart: 11, of which 5 were waited for; matrix products, arithmetic and copies ran while one was open for 16% of the time, Pallas kernels for 0%

commit v1 on v0

--- a/solution.py
+++ b/solution.py
@@ -64,7 +64,9 @@
 
 
 def apply_coarse(field, coarse_diagonal, coarse_columns, coarse_blocks):
-    gathered = lax.all_gather(field, DOM, axis=0, tiled=True)
+    heard = jnp.stack([field for _ in range(lax.axis_size(DOM))])
+    u_next = lax.all_to_all(heard, DOM, split_axis=0, concat_axis=0)
+    gathered = jnp.concatenate(u_next, 0)
     nearby = gathered[coarse_columns]
     return coarse_diagonal * field - couple(coarse_blocks, nearby)
 

time: 764 us -> 675 us (0.88)
  blocking collectives: 182 us -> 45.2 us
  starting transfers between devices: 49.7 us -> 74.8 us
  waiting for transfers between devices: 27.8 us -> 48.4 us
    all_gather x5 -> x0, blocking collectives: 168 us -> none  [apply_coarse(): gathered = lax.all_gather(field, DOM, axis=0, tiled=True)]
    all_to_all x0 -> x2, blocking collectives: none -> 30.6 us  [apply_coarse(): u_next = lax.all_to_all(heard, DOM, split_axis=0, concat_axis=0)]
    all_to_all x0 -> x3, starting transfers between devices: none -> 25 us  [apply_coarse(): u_next = lax.all_to_all(heard, DOM, split_axis=0, concat_axis=0)]
    all_to_all x0 -> x3, waiting for transfers between devices: none -> 20.5 us  [apply_coarse(): u_next = lax.all_to_all(heard, DOM, split_axis=0, concat_axis=0)]
  transfers between devices with their start and end apart: 11 -> 14, of which waited for: 5 -> 8; matrix products, arithmetic and copies ran while one was open for 16% -> 18% of each run, Pallas kernels for 0% -> 0%
where the time goes in v1:
time: 675 us; the launch traced here: 674 us
  local copies, waits for them, and re-layouts  484 us (72%)
  starting transfers between devices  74.8 us (11%)
  waiting for transfers between devices  48.4 us (7%)
  blocking collectives  45.2 us (7%)
  other arithmetic  18.7 us (3%)
    gather x16, local copies, waits for them, and re-layouts, apply_fine(): nearby = padded[local_columns]  418 us
    all_to_all x2, blocking collectives, apply_coarse(): u_next = lax.all_to_all(heard, DOM, split_axis=0, concat_axis=0)  30.6 us
    all_to_all x3, starting transfers between devices, turned_blocks(): whole = lax.all_to_all(whole, axes[k], k, k, tiled=True)  26.9 us
    all_to_all x3, starting transfers between devices, apply_coarse(): u_next = lax.all_to_all(heard, DOM, split_axis=0, concat_axis=0)  25 us
    split x270, local copies, waits for them, and re-layouts, split_up(): return jnp.stack(jnp.split(value, peers, axis=dim))  20.8 us
    all_to_all x3, waiting for transfers between devices, apply_coarse(): u_next = lax.all_to_all(heard, DOM, split_axis=0, concat_axis=0)  20.5 us
    ppermute x4, waiting for transfers between devices, padded_2(): after = lax.ppermute(initial, axis, down)  15.1 us
    all_to_all x3, blocking collectives, turned_blocks(): whole = lax.all_to_all(whole, axes[k], k, k, tiled=True)  14.6 us
  transfers between devices with their start and end apart: 14, of which 8 were waited for; matrix products, arithmetic and copies ran while one was open for 18% of the time, Pallas kernels for 0%

profile of v1, /device:TPU:103, one launch (start us, length us, event | category | flops | bytes accessed | tf_op | source)
XLA Modules:
  0.0 673.5 jit_solution(5358940583372504667)
XLA Ops:
  8.2 9.7 %stack.912 = s32[128,8]{1,0:T(8,128)} concatenate(s32[1,8]{1,0:T(1,128)S(1)} %get-tuple-element.405, s32[1,8]{1,0:T(1,128)S(1)} %get-tuple-element.404, s32[1,8]{1,0:T(1,128)S(1)} %get-tuple-element.403, s32[1,8]{1,0:T(1,128)S(1)} %get-tuple-element.402, s32[1,8]{1,0:T(1,128)S(1)} %get-tuple-element.401, s32[1,8]{1,0:T(1,128)S(1)} %get-tuple-element.400, ...), dimensions={0} | concatenate | bytes 8192 | tf_op jit(solution)/shard_map/stack | solution.py:30
  17.9 10.3 %all-to-all-start = ((s32[64,2,8]{2,1,0:T(2,128)}), s32[64,2,8]{2,1,0:T(2,128)S(1)}, u32[]{:S(2)}, u32[]{:S(2)}) async-start(s32[64,2,8]{2,1,0:T(2,128)} %bitcast.128), calls=%async_computation | async-start | bytes 131072 | tf_op jit(solution)/shard_map/all_to_all | solution.py:43
  30.1 91.5 %gather_fusion = f32[27648,3]{1,0:T(8,128)} fusion(f32[1536,3]{1,0:T(8,128)S(1)} %copy.2696, s32[27648]{0:T(1024)S(1)} %broadcast_clamp_fusion), kind=kCustom, calls=%fused_computation | custom fusion | bytes 774144 | tf_op jit(solution)/shard_map/gather | solution.py:62
  121.6 8.3 %copy.2697 = f32[27648,3]{0,1:T(4,128)S(1)} copy(f32[27648,3]{1,0:T(8,128)} %gather_fusion) | data formatting | bytes 663552 | tf_op jit(solution)/shard_map/gather | solution.py:62
  148.9 91.5 %gather_fusion.1 = f32[27648,3]{1,0:T(8,128)} fusion(f32[1536,3]{1,0:T(8,128)S(1)} %copy.2702, s32[27648]{0:T(1024)S(1)} %broadcast_clamp_fusion), kind=kCustom, calls=%fused_computation.1 | custom fusion | bytes 774144 | tf_op jit(solution)/shard_map/gather | solution.py:62
  240.4 8.3 %copy.2703 = f32[27648,3]{0,1:T(4,128)S(1)} copy(f32[27648,3]{1,0:T(8,128)} %gather_fusion.1) | data formatting | bytes 663552 | tf_op jit(solution)/shard_map/gather | solution.py:62
  273.8 8.9 %all-to-all-start.2 = ((f32[64,2,8,3]{2,1,3,0:T(2,128)}), f32[64,2,8,3]{2,1,3,0:T(2,128)S(1)}, u32[]{:S(2)}, u32[]{:S(2)}) async-start(f32[64,2,8,3]{2,1,3,0:T(2,128)} %copy.2835), calls=%async_computation.2 | async-start | bytes 393216 | tf_op jit(solution)/shard_map/all_to_all | solution.py:43
  282.7 6.5 all-to-all-done.2
  302.7 7.8 %all-to-all-start.4 = ((f32[128,32,3]{1,2,0:T(4,128)}), f32[128,32,3]{1,2,0:T(4,128)S(1)}, u32[]{:S(2)}, u32[]{:S(2)}) async-start(f32[128,32,3]{1,2,0:T(4,128)} %stack.2074), calls=%async_computation.4 | async-start | bytes 524288 | tf_op jit(solution)/shard_map/all_to_all | solution.py:68
  310.6 6.9 %all-to-all-done.4 = f32[128,32,3]{1,2,0:T(4,128)S(1)} async-done(((f32[128,32,3]{1,2,0:T(4,128)}), f32[128,32,3]{1,2,0:T(4,128)S(1)}, u32[]{:S(2)}, u32[]{:S(2)}) %all-to-all-start.4) | async-done | bytes 49184 | tf_op jit(solution)/shard_map/all_to_all | solution.py:68
  320.7 15.3 %all_to_all.57 = f32[128,32,3]{1,2,0:T(4,128)S(1)} all-to-all(f32[128,32,3]{1,2,0:T(4,128)S(1)} %stack.2075), channel_id=1, replica_groups=mesh['dom_0'=4,'dom_1'=4,'dom_2'=4,'dom_3'=2] {'dom_0','dom_1','dom_2','..., dimensions={0} | all-to-all | bytes 98304 | tf_op jit(solution)/shard_map/all_to_all | solution.py:68
  339.2 15.3 %all_to_all.58 = f32[128,32,3]{1,2,0:T(4,128)S(1)} all-to-all(f32[128,32,3]{1,2,0:T(4,128)S(1)} %stack.2076), channel_id=1, replica_groups=mesh['dom_0'=4,'dom_1'=4,'dom_2'=4,'dom_3'=2] {'dom_0','dom_1','dom_2','..., dimensions={0} | all-to-all | bytes 98304 | tf_op jit(solution)/shard_map/all_to_all | solution.py:68
  358.4 8.6 %all-to-all-start.7 = ((f32[128,32,3]{1,2,0:T(4,128)}), f32[128,32,3]{1,2,0:T(4,128)S(1)}, u32[]{:S(2)}, u32[]{:S(2)}) async-start(f32[128,32,3]{1,2,0:T(4,128)} %stack.2077), calls=%async_computation.7 | async-start | bytes 524288 | tf_op jit(solution)/shard_map/all_to_all | solution.py:68
  367.1 6.8 %all-to-all-done.7 = f32[128,32,3]{1,2,0:T(4,128)S(1)} async-done(((f32[128,32,3]{1,2,0:T(4,128)}), f32[128,32,3]{1,2,0:T(4,128)S(1)}, u32[]{:S(2)}, u32[]{:S(2)}) %all-to-all-start.7) | async-done | bytes 49184 | tf_op jit(solution)/shard_map/all_to_all | solution.py:68
  377.7 8.6 %all-to-all-start.8 = ((f32[128,32,3]{1,2,0:T(4,128)}), f32[128,32,3]{1,2,0:T(4,128)S(1)}, u32[]{:S(2)}, u32[]{:S(2)}) async-start(f32[128,32,3]{1,2,0:T(4,128)} %stack.2078), calls=%async_computation.8 | async-start | bytes 524288 | tf_op jit(solution)/shard_map/all_to_all | solution.py:68
  386.3 6.9 %all-to-all-done.8 = f32[128,32,3]{1,2,0:T(4,128)S(1)} async-done(((f32[128,32,3]{1,2,0:T(4,128)}), f32[128,32,3]{1,2,0:T(4,128)S(1)}, u32[]{:S(2)}, u32[]{:S(2)}) %all-to-all-start.8) | async-done | bytes 49184 | tf_op jit(solution)/shard_map/all_to_all | solution.py:68
  412.3 7.7 %all-to-all-start.9 = ((f32[64,2,8,3]{2,1,3,0:T(2,128)}), f32[64,2,8,3]{2,1,3,0:T(2,128)S(1)}, u32[]{:S(2)}, u32[]{:S(2)}) async-start(f32[64,2,8,3]{2,1,3,0:T(2,128)} %copy.2985), calls=%async_computation.9 | async-start | bytes 393216 | tf_op jit(solution)/shard_map/all_to_all | solution.py:43
  420.0 6.3 all-to-all-done.9
  444.4 7.2 %collective-permute-done.5 = f32[256,3]{0,1:T(4,128)S(1)} collective-permute-done((f32[256,3]{0,1:T(4,128)S(1)}, f32[256,3]{0,1:T(4,128)S(1)}, u32[]{:S(2)}, u32[]{:S(2)}) %collective-permute-start.5) | collective-permute-done | bytes 3104 | tf_op jit(solution)/shard_map/ppermute | solution.py:24
  451.9 91.5 %gather_fusion.10 = f32[27648,3]{1,0:T(8,128)} fusion(f32[1536,3]{1,0:T(8,128)S(1)} %copy.2989, s32[27648]{0:T(1024)S(1)} %broadcast_clamp_fusion), kind=kCustom, calls=%fused_computation.10 | custom fusion | bytes 774144 | tf_op jit(solution)/shard_map/gather | solution.py:62
  543.3 8.3 %copy.2990 = f32[27648,3]{0,1:T(4,128)S(1)} copy(f32[27648,3]{1,0:T(8,128)} %gather_fusion.10) | data formatting | bytes 663552 | tf_op jit(solution)/shard_map/gather | solution.py:62
  561.3 6.5 collective-permute-done.7
  568.1 91.5 %gather_fusion.11 = f32[27648,3]{1,0:T(8,128)} fusion(f32[1536,3]{1,0:T(8,128)S(1)} %copy.2992, s32[27648]{0:T(1024)S(1)} %broadcast_clamp_fusion), kind=kCustom, calls=%fused_computation.11 | custom fusion | bytes 774144 | tf_op jit(solution)/shard_map/gather | solution.py:62
  659.6 8.3 %copy.2993 = f32[27648,3]{0,1:T(4,128)S(1)} copy(f32[27648,3]{1,0:T(8,128)} %gather_fusion.11) | data formatting | bytes 663552 | tf_op jit(solution)/shard_map/gather | solution.py:62
  (682 shorter events, 133.1 us)
Async XLA Ops:
  1.4 28.4 %collective-permute-start = (f32[256,3]{0,1:T(4,128)S(1)}, f32[256,3]{0,1:T(4,128)S(1)}, u32[]{:S(2)}, u32[]{:S(2)}) collective-permute-start(f32[256,3]{0,1:T(4,128)S(1)} %get-tuple-element.276), channel_id=1, source_target_pairs={{0,1},{1,2},{2,3},{3,4},{4,5},{5,6},{6,7},{7,8},{8,9},{9,10},{10,1... | collective-permute-start | bytes 9224 | tf_op jit(solution)/shard_map/ppermute | solution.py:23
  3.7 26.1 %collective-permute-start.1 = (f32[256,3]{0,1:T(4,128)S(1)}, f32[256,3]{0,1:T(4,128)S(1)}, u32[]{:S(2)}, u32[]{:S(2)}) collective-permute-start(f32[256,3]{0,1:T(4,128)S(1)} %get-tuple-element.277), channel_id=1, source_target_pairs={{1,0},{2,1},{3,2},{4,3},{5,4},{6,5},{7,6},{8,7},{9,8},{10,9},{11,1... | collective-permute-start | bytes 9224 | tf_op jit(solution)/shard_map/ppermute | solution.py:24
  17.9 123.6 %all-to-all-start = ((s32[64,2,8]{2,1,0:T(2,128)}), s32[64,2,8]{2,1,0:T(2,128)S(1)}, u32[]{:S(2)}, u32[]{:S(2)}) async-start(s32[64,2,8]{2,1,0:T(2,128)} %bitcast.128), calls=%async_computation | async-start | bytes 131072 | tf_op jit(solution)/shard_map/all_to_all | solution.py:43
  129.8 4.9 copy-start
  132.8 2.1 copy-start.3
  132.8 2.1 copy-start.4
  132.8 8.6 %copy-start.6 = (s32[32,27]{1,0:T(8,128)S(1)}, s32[32,27]{1,0:T(8,128)}, u32[]{:S(2)}) copy-start(s32[32,27]{1,0:T(8,128)} %param.16) | copy-start | bytes 10372
  135.0 12.2 %collective-permute-start.2 = (f32[256,3]{0,1:T(4,128)S(1)}, f32[256,3]{0,1:T(4,128)S(1)}, u32[]{:S(2)}, u32[]{:S(2)}) collective-permute-start(f32[256,3]{0,1:T(4,128)S(1)} %get-tuple-element.274), channel_id=1, source_target_pairs={{0,1},{1,2},{2,3},{3,4},{4,5},{5,6},{6,7},{7,8},{8,9},{9,10},{10,1... | collective-permute-start | bytes 9224 | tf_op jit(solution)/shard_map/ppermute | solution.py:23
  139.5 9.1 %collective-permute-start.3 = (f32[256,3]{0,1:T(4,128)S(1)}, f32[256,3]{0,1:T(4,128)S(1)}, u32[]{:S(2)}, u32[]{:S(2)}) collective-permute-start(f32[256,3]{0,1:T(4,128)S(1)} %get-tuple-element.275), channel_id=1, source_target_pairs={{1,0},{2,1},{3,2},{4,3},{5,4},{6,5},{7,6},{8,7},{9,8},{10,9},{11,1... | collective-permute-start | bytes 9224 | tf_op jit(solution)/shard_map/ppermute | solution.py:24
  251.6 2.3 copy-start.8
  261.0 41.0 %copy-start.5 = (f32[32,3]{0,1:T(4,128)S(1)}, f32[32,3]{0,1:T(4,128)}, u32[]{:S(2)}) copy-start(f32[32,3]{0,1:T(4,128)} %param.15) | copy-start | bytes 1156
  273.8 15.4 %all-to-all-start.2 = ((f32[64,2,8,3]{2,1,3,0:T(2,128)}), f32[64,2,8,3]{2,1,3,0:T(2,128)S(1)}, u32[]{:S(2)}, u32[]{:S(2)}) async-start(f32[64,2,8,3]{2,1,3,0:T(2,128)} %copy.2835), calls=%async_computation.2 | async-start | bytes 393216 | tf_op jit(solution)/shard_map/all_to_all | solution.py:43
  302.7 14.7 %all-to-all-start.4 = ((f32[128,32,3]{1,2,0:T(4,128)}), f32[128,32,3]{1,2,0:T(4,128)S(1)}, u32[]{:S(2)}, u32[]{:S(2)}) async-start(f32[128,32,3]{1,2,0:T(4,128)} %stack.2074), calls=%async_computation.4 | async-start | bytes 524288 | tf_op jit(solution)/shard_map/all_to_all | solution.py:68
  318.3 2.2 copy-start.2
  358.4 15.5 %all-to-all-start.7 = ((f32[128,32,3]{1,2,0:T(4,128)}), f32[128,32,3]{1,2,0:T(4,128)S(1)}, u32[]{:S(2)}, u32[]{:S(2)}) async-start(f32[128,32,3]{1,2,0:T(4,128)} %stack.2077), calls=%async_computation.7 | async-start | bytes 524288 | tf_op jit(solution)/shard_map/all_to_all | solution.py:68
  377.7 15.5 %all-to-all-start.8 = ((f32[128,32,3]{1,2,0:T(4,128)}), f32[128,32,3]{1,2,0:T(4,128)S(1)}, u32[]{:S(2)}, u32[]{:S(2)}) async-start(f32[128,32,3]{1,2,0:T(4,128)} %stack.2078), calls=%async_computation.8 | async-start | bytes 524288 | tf_op jit(solution)/shard_map/all_to_all | solution.py:68
  396.4 2.9 copy-start.7
  412.3 13.9 %all-to-all-start.9 = ((f32[64,2,8,3]{2,1,3,0:T(2,128)}), f32[64,2,8,3]{2,1,3,0:T(2,128)S(1)}, u32[]{:S(2)}, u32[]{:S(2)}) async-start(f32[64,2,8,3]{2,1,3,0:T(2,128)} %copy.2985), calls=%async_computation.9 | async-start | bytes 393216 | tf_op jit(solution)/shard_map/all_to_all | solution.py:43
  437.0 7.4 %collective-permute-start.4 = (f32[256,3]{0,1:T(4,128)S(1)}, f32[256,3]{0,1:T(4,128)S(1)}, u32[]{:S(2)}, u32[]{:S(2)}) collective-permute-start(f32[256,3]{0,1:T(4,128)S(1)} %get-tuple-element.272), channel_id=1, source_target_pairs={{0,1},{1,2},{2,3},{3,4},{4,5},{5,6},{6,7},{7,8},{8,9},{9,10},{10,1... | collective-permute-start | bytes 9224 | tf_op jit(solution)/shard_map/ppermute | solution.py:23
  442.4 9.1 %collective-permute-start.5 = (f32[256,3]{0,1:T(4,128)S(1)}, f32[256,3]{0,1:T(4,128)S(1)}, u32[]{:S(2)}, u32[]{:S(2)}) collective-permute-start(f32[256,3]{0,1:T(4,128)S(1)} %get-tuple-element.273), channel_id=1, source_target_pairs={{1,0},{2,1},{3,2},{4,3},{5,4},{6,5},{7,6},{8,7},{9,8},{10,9},{11,1... | collective-permute-start | bytes 9224 | tf_op jit(solution)/shard_map/ppermute | solution.py:24
  551.6 4.9 copy-start.1
  556.7 4.6 collective-permute-start.6
  558.7 9.1 %collective-permute-start.7 = (f32[256,3]{0,1:T(4,128)S(1)}, f32[256,3]{0,1:T(4,128)S(1)}, u32[]{:S(2)}, u32[]{:S(2)}) collective-permute-start(f32[256,3]{0,1:T(4,128)S(1)} %get-tuple-element.271), channel_id=1, source_target_pairs={{1,0},{2,1},{3,2},{4,3},{5,4},{6,5},{7,6},{8,7},{9,8},{10,9},{11,1... | collective-permute-start | bytes 9224 | tf_op jit(solution)/shard_map/ppermute | solution.py:24
